TPU v7x, 32 devices: a whole 2x2x4 slice. The times are simulated.
32 devices in a mesh: row: 8 (over y, x, core), col: 4 (over z).
Axes of the slice: x: 2, y: 2, z: 4, core: 2. Of those that a mesh axis runs over, the one named last changes fastest.
Arguments:
- surface: bfloat16 [16384, 16384], P('row', 'col'), may hold values from -0.0234375 to 0.0234375
- excitation: float32 [16384, 128], P(('row', 'col')), may hold values from -6 to 6
- dtn_blocks: bfloat16 [32, 1024, 1024], P(('row', 'col')), may hold values from -0.09375 to 0.09375
- interp_blocks: bfloat16 [32, 1024, 2048], P(('row', 'col')), may hold values from -0.09375 to 0.09375
- adjacency: int32 [32, 6], P(('row', 'col')), may hold values from 0 to 31, as said below
Outputs:
- solution: float32 [16384, 128], P(('row', 'col'))
- residual: float32 [16384, 128], P(('row', 'col'))
Inputs may be any that keep to these rules, and one draw needn't show every extreme that they name: `adjacency`: entry [s, k] names a subdomain of the same spatial group as s (equal index // 4); it may name s itself, which adds nothing.
All inputs are finite; a program needn't handle non-finite values.
Results may differ from a plain program's by a relative error of at most 0.02.
Values may be sent and summed in bfloat16 or wider, within the bound.
A program may use at most 64 MiB of HBM per device.

v0:
```python
import jax
import jax.numpy as jnp
from jax import lax
from jax.sharding import PartitionSpec as P

ITERS = 2
NADJ = 6
damping = 0.25
face_weight = 0.25


def broadcast(value, axis, source):
    kept = jnp.where(lax.axis_index(axis) == source, value, 0).astype(value.dtype)
    return lax.psum(kept, axis)


def local(surface, excitation, dtn_blocks, interp_blocks, adjacency):
    col_count = lax.axis_size("col")
    row_count = lax.axis_size("row")
    col_index = lax.axis_index("col")
    dtn_block = dtn_blocks[0]
    interp_block = interp_blocks[0]
    local_adjacent = adjacency[0] % col_count
    current = excitation
    residual = excitation
    for sweep in range(ITERS):
        rounded = current.astype(jnp.bfloat16)
        group_block = lax.all_gather(rounded, "col", axis=0, tiled=True)
        per_column = row_count // col_count
        received = [
            broadcast(group_block, "row", col_index * per_column + member)
            for member in range(per_column)
        ]
        column_block = jnp.concatenate(received, axis=0)
        traces = jnp.dot(interp_block, group_block, preferred_element_type=jnp.float32).astype(
            jnp.bfloat16
        )
        segment = lax.all_gather(traces[None], "col", axis=0, tiled=True)
        owners = jnp.arange(segment.shape[0], dtype=jnp.int32)
        counts = jnp.sum((local_adjacent[None, :] == owners[:, None]).astype(jnp.float32), axis=1)
        neighbours = jnp.einsum(
            "p,pmn->mn", counts.astype(jnp.bfloat16), segment, preferred_element_type=jnp.float32
        )
        own_wide = traces.astype(jnp.float32)
        combined = jnp.dot(dtn_block, traces, preferred_element_type=jnp.float32) + own_wide
        combined = combined + face_weight * (NADJ * own_wide - neighbours)
        response = combined.astype(jnp.bfloat16)
        surface_part = jnp.dot(surface, column_block, preferred_element_type=jnp.float32)
        volume_part = lax.dot_general(
            interp_block, response, (((0,), (0,)), ((), ())), preferred_element_type=jnp.float32
        )
        summed = lax.psum_scatter(
            (surface_part + volume_part).astype(jnp.bfloat16),
            "col",
            scatter_dimension=0,
            tiled=True,
        ).astype(jnp.float32)
        residual = excitation - current - summed
        current = current + damping * residual
    return (current, residual)


def solution(mesh):
    in_specs = (
        P("row", "col"),
        P(("row", "col"), None),
        P(("row", "col"), None, None),
        P(("row", "col"), None, None),
        P(("row", "col"), None),
    )
    out_specs = (P(("row", "col"), None), P(("row", "col"), None))
    return jax.shard_map(local, mesh=mesh, in_specs=in_specs, out_specs=out_specs, check_vma=False)
```

profile of v0, /device:TPU:0, one launch (start us, length us, event | category | flops | bytes accessed | tf_op | source)
XLA Modules:
  0.0 250.6 jit_solution(15848962410064258992)
XLA Ops:
  8.0 0.0 copy-start
  8.0 0.0 all-reduce.7.cloned.1.call-start
  8.1 1.2 copy.18
  9.3 17.4 %all_gather.12 = bf16[2048,128]{0,1:T(8,128)(2,1)S(1)} all-gather(bf16[512,128]{0,1:T(8,128)(2,1)S(1)} %convert_element_type.58), channel_id=1, replica_groups=mesh['row'=8,'col'=4] {'col'}, dimensions={0}, use_global_device_ids=true | all-gather | bytes 655360 | tf_op jit(solution)/shard_map/all_gather | solution.py:28
  26.7 1.0 broadcast_select_fusion.3
  27.7 0.0 copy-start.2
  27.7 0.0 all-reduce.7.cloned.1.call-update
  27.8 0.0 all-gather.5.cloned.1.call-start
  27.8 4.1 %fusion.54 = bf16[1024,128]{1,0:T(8,128)(2,1)} fusion(bf16[2048,128]{0,1:T(8,128)(2,1)S(1)} %all_gather.12, bf16[1,1024,2048]{2,1,0:T(8,128)(2,1)} %param.8), kind=kOutput, calls=%fused_computation.26 | convolution fusion | flops 537001984 | bytes 4980736 | tf_op jit(solution)/shard_map/dot_general | solution.py:35
  32.0 0.0 all-gather.5.cloned.1.call-update
  32.0 0.0 reduce-scatter.3.cloned.1.call-start
  32.0 0.0 copy-done.2
  32.1 0.1 convert_reduce_fusion
  32.2 54.3 %all-reduce.7.cloned.1.call-done = (bf16[2048,128]{0,1:T(8,128)(2,1)}, bf16[2048,128]{0,1:T(8,128)(2,1)}) async-done(((bf16[2048,128]{0,1:T(8,128)(2,1)}, bf16[2048,128]{0,1:T(8,128)(2,1)}), (bf16[2048,128]{0,1:T(8,128)(2,1)}, bf16[2048,128]{0,1:T(8,128)(2,1)})) %all-reduce.7.cloned.1.call-update) | async-done | bytes 1048592 | tf_op jit(solution)/shard_map/psum | solution.py:14
  86.4 11.8 %fusion.60 = f32[128,2048]{1,0:T(8,128)S(1)} fusion(bf16[2048,4096]{1,0:T(8,128)(2,1)} %param.5, bf16[2048,128]{0,1:T(8,128)(2,1)} %get-tuple-element.8, bf16[2048,128]{0,1:T(8,128)(2,1)} %get-tuple-element.9), kind=kOutput, calls=%fused_computation.28 | convolution fusion | flops 2149580800 | bytes 18874368 | tf_op jit(solution)/shard_map/dot_general | solution.py:48
  98.2 0.0 all-gather.5.cloned.1.call-done
  98.2 3.0 %fusion.70 = f32[1,1024,128]{2,0,1:T(1,128)} fusion(bf16[4,1024,128]{2,1,0:T(8,128)(2,1)} %bitcast.101, bf16[4]{0:T(256)(128)(2,1)S(1)} %convert_reduce_fusion), kind=kOutput, calls=%fused_computation.38 | convolution fusion | flops 1048576 | bytes 1572872 | tf_op jit(solution)/shard_map/p,pmn->mn/dot_general | solution.py:41
  101.2 0.0 copy-done
  101.2 4.6 %fusion.20 = bf16[2048,128]{0,1:T(8,128)(2,1)} fusion(f32[128,2048]{1,0:T(8,128)S(1)} %fusion.60, bf16[1,1024,2048]{2,1,0:T(8,128)(2,1)} %param.8, bf16[1024,128]{1,0:T(8,128)(2,1)} %fusion.54, bf16[1,1024,1024]{2,1,0:T(8,128)(2,1)S(1)} %copy-done, f32[1024,128]{1,0:T(8,128)} %bitcast.100), kind=kOutput, calls=%fused_computation.12 | convolution fusion | flops 806748160 | bytes 8650752 | tf_op jit(solution)/shard_map/dot_general | solution.py:49
  105.8 0.0 reduce-scatter.3.cloned.1.call-update
  105.8 0.0 all-reduce.5.cloned.1.call-start
  105.8 21.1 %reduce-scatter.3.cloned.1.call-done = bf16[512,128]{0,1:T(8,128)(2,1)} async-done(((bf16[2048,128]{0,1:T(8,128)(2,1)}), bf16[512,128]{0,1:T(8,128)(2,1)}) %reduce-scatter.3.cloned.1.call-update) | async-done | bytes 131088 | tf_op jit(solution)/shard_map/reduce_scatter | solution.py:52
  127.0 1.0 fusion.88
  127.9 15.3 %all_gather.14 = bf16[2048,128]{0,1:T(8,128)(2,1)S(1)} all-gather(bf16[512,128]{0,1:T(8,128)(2,1)S(1)} %fusion.88), channel_id=1, replica_groups=mesh['row'=8,'col'=4] {'col'}, dimensions={0}, use_global_device_ids=true | all-gather | bytes 655360 | tf_op jit(solution)/shard_map/all_gather | solution.py:28
  143.2 1.0 broadcast_select_fusion.2
  144.3 0.0 all-reduce.5.cloned.1.call-update
  144.3 0.0 all-gather.7.cloned.1.call-start
  144.3 4.1 %fusion.57 = bf16[128,1024]{0,1:T(8,128)(2,1)} fusion(bf16[2048,128]{0,1:T(8,128)(2,1)S(1)} %all_gather.14, bf16[1,1024,2048]{2,1,0:T(8,128)(2,1)} %param.8), kind=kOutput, calls=%fused_computation.27 | convolution fusion | flops 537001984 | bytes 4980736 | tf_op jit(solution)/shard_map/dot_general | solution.py:35
  148.5 0.0 all-gather.7.cloned.1.call-update
  148.5 0.2 reduce-scatter.5.cloned.1.call-start
  148.7 51.0 %all-reduce.5.cloned.1.call-done = (bf16[2048,128]{0,1:T(8,128)(2,1)}, bf16[2048,128]{0,1:T(8,128)(2,1)}) async-done(((bf16[2048,128]{0,1:T(8,128)(2,1)}, bf16[2048,128]{0,1:T(8,128)(2,1)}), (bf16[2048,128]{0,1:T(8,128)(2,1)}, bf16[2048,128]{0,1:T(8,128)(2,1)})) %all-reduce.5.cloned.1.call-update) | async-done | bytes 1048592 | tf_op jit(solution)/shard_map/psum | solution.py:14
  199.7 11.8 %fusion.64 = f32[128,2048]{1,0:T(8,128)S(1)} fusion(bf16[2048,4096]{1,0:T(8,128)(2,1)} %param.5, bf16[2048,128]{0,1:T(8,128)(2,1)} %get-tuple-element.6, bf16[2048,128]{0,1:T(8,128)(2,1)} %get-tuple-element.7), kind=kOutput, calls=%fused_computation.32 | convolution fusion | flops 2149580800 | bytes 18874368 | tf_op jit(solution)/shard_map/dot_general | solution.py:48
  211.5 0.0 all-gather.7.cloned.1.call-done
  211.5 3.0 %fusion.68 = f32[1,1024,128]{2,0,1:T(1,128)} fusion(bf16[4,1024,128]{2,1,0:T(8,128)(2,1)} %bitcast.102, bf16[4]{0:T(256)(128)(2,1)S(1)} %convert_reduce_fusion), kind=kOutput, calls=%fused_computation.36 | convolution fusion | flops 1048576 | bytes 1572872 | tf_op jit(solution)/shard_map/p,pmn->mn/dot_general | solution.py:41
  214.5 0.0 copy-start.1
  214.5 4.6 %fusion.23 = bf16[2048,128]{0,1:T(8,128)(2,1)} fusion(f32[128,2048]{1,0:T(8,128)S(1)} %fusion.64, bf16[1,1024,2048]{2,1,0:T(8,128)(2,1)} %param.8, bf16[128,1024]{0,1:T(8,128)(2,1)} %fusion.57, bf16[1,1024,1024]{2,1,0:T(8,128)(2,1)S(1)} %copy-done, f32[1024,128]{1,0:T(8,128)} %bitcast.99), kind=kOutput, calls=%fused_computation.13 | convolution fusion | flops 806748160 | bytes 8650752 | tf_op jit(solution)/shard_map/dot_general | solution.py:49
  219.1 0.0 reduce-scatter.5.cloned.1.call-update
  219.1 21.2 %reduce-scatter.5.cloned.1.call-done = bf16[512,128]{0,1:T(8,128)(2,1)} async-done(((bf16[2048,128]{0,1:T(8,128)(2,1)}), bf16[512,128]{0,1:T(8,128)(2,1)}) %reduce-scatter.5.cloned.1.call-update) | async-done | bytes 131088 | tf_op jit(solution)/shard_map/reduce_scatter | solution.py:52
  240.3 0.0 copy-done.1
  240.3 1.0 convert_subtract_fusion
  241.3 0.8 copy.22
  242.1 0.8 copy.21
  (2 shorter events, 0.0 us)
Async XLA Ops:
  8.0 93.2 %copy-start = (bf16[1,1024,1024]{2,1,0:T(8,128)(2,1)S(1)}, bf16[1,1024,1024]{2,1,0:T(8,128)(2,1)}, u32[]{:S(2)}) copy-start(bf16[1,1024,1024]{2,1,0:T(8,128)(2,1)} %param.7) | copy-start | bytes 6291460
  8.0 78.4 %all-reduce.7.cloned.1.call-start = ((), (), s32[]{:S(2)}) async-start(), calls=%async_computation.7 | async-start | bytes 2097152 | tf_op jit(solution)/shard_map/psum | solution.py:14
  27.7 4.3 %copy-start.2 = (s32[1,6]{1,0:T(1,128)S(1)}, s32[1,6]{1,0:T(1,128)}, u32[]{:S(2)}) copy-start(s32[1,6]{1,0:T(1,128)} %param.9) | copy-start | bytes 76
  27.8 70.5 %all-gather.5.cloned.1.call-start = ((), (), s32[]{:S(2)}) async-start(), calls=%async_computation.4 | async-start | bytes 1310720 | tf_op jit(solution)/shard_map/all_gather | solution.py:38
  32.0 95.0 %reduce-scatter.3.cloned.1.call-start = ((), (), s32[]{:S(2)}) async-start(), calls=%async_computation.2 | async-start | bytes 655360 | tf_op jit(solution)/shard_map/reduce_scatter | solution.py:52
  105.8 93.9 %all-reduce.5.cloned.1.call-start = ((), (), s32[]{:S(2)}) async-start(), calls=%async_computation.6 | async-start | bytes 2097152 | tf_op jit(solution)/shard_map/psum | solution.py:14
  144.3 67.2 %all-gather.7.cloned.1.call-start = ((), (), s32[]{:S(2)}) async-start(), calls=%async_computation.5 | async-start | bytes 1310720 | tf_op jit(solution)/shard_map/all_gather | solution.py:38
  148.5 91.8 %reduce-scatter.5.cloned.1.call-start = ((), (), s32[]{:S(2)}) async-start(), calls=%async_computation.3 | async-start | bytes 655360 | tf_op jit(solution)/shard_map/reduce_scatter | solution.py:52
  214.5 25.8 %copy-start.1 = (bf16[512,128]{0,1:T(8,128)(2,1)S(1)}, bf16[512,128]{0,1:T(8,128)(2,1)}, u32[]{:S(2)}) copy-start(bf16[512,128]{0,1:T(8,128)(2,1)} %reduce-scatter.3.cloned.1.call-done) | copy-start | bytes 393220
Sparse Core Ops, SparseCore 0:
  27.9 58.5 all-reduce.6
  144.4 55.2 all-reduce.4
Sparse Core Ops, SparseCore 1:
  32.1 29.6 all-gather.4
  105.9 21.0 reduce-scatter.2
  148.6 26.4 all-gather.6
  219.2 21.0 reduce-scatter.4
where the time goes:
time: 251 us
  waiting for transfers between devices  148 us (59%)
  matrix products  46.9 us (19%)
  blocking collectives  32.7 us (13%)
  between operations  15.8 us (6%)
  other arithmetic  4.18 us (2%)
  local copies, waits for them, and re-layouts  2.9 us (1%)
    psum x2, waiting for transfers between devices, broadcast(): return lax.psum(kept, axis)  105 us
    reduce_scatter x2, waiting for transfers between devices, local(): lax.psum_scatter((surface_part + volume_part).astype(jnp.bfloat16), 'col'...  42.3 us
    all_gather x2, blocking collectives, local(): group_block = lax.all_gather(rounded, 'col', axis=0, tiled=True)  32.7 us
    dot_general x2, matrix products, local(): jnp.dot(surface, column_block, preferred_element_type=jnp.float32)  23.5 us
    dot_general x2, matrix products, local(): lax.dot_general(interp_block, response, (((0,), (0,)), ((), ())), preferr...  9.18 us
    dot_general x2, matrix products, local(): jnp.dot(interp_block, group_block, preferred_element_type=jnp.float32)  8.29 us
    dot_general x2, matrix products, local(): jnp.einsum('p,pmn->mn', counts.astype(jnp.bfloat16), segment, preferred_e...  5.92 us
  transfers between devices with their start and end apart: 6, of which 4 were waited for; matrix products, arithmetic and copies ran while one was open for 13% of the time, Pallas kernels for 0%

commit v1 on v0

--- a/solution.py
+++ b/solution.py
@@ -7,6 +7,12 @@
 NADJ = 6
 damping = 0.25
 face_weight = 0.25
+
+
+def match_the_paths(local_block, dev_axis):
+    v1 = jnp.stack([local_block for _ in range(lax.axis_size(dev_axis))])
+    d_next = lax.all_to_all(v1, axis_name=dev_axis, split_axis=0, concat_axis=0)
+    return jnp.concatenate(d_next, axis=0)
 
 
 def broadcast(value, axis, source):
@@ -25,7 +31,7 @@
     residual = excitation
     for sweep in range(ITERS):
         rounded = current.astype(jnp.bfloat16)
-        group_block = lax.all_gather(rounded, "col", axis=0, tiled=True)
+        group_block = match_the_paths(rounded, "col")
         per_column = row_count // col_count
         received = [
             broadcast(group_block, "row", col_index * per_column + member)

time: 251 us -> 254 us (1.012)
  blocking collectives: 32.7 us -> 15.5 us
  waiting for transfers between devices: 148 us -> 159 us
  starting transfers between devices: 0.44 us -> 6.75 us
    all_gather x2 -> x0, blocking collectives: 32.7 us -> none  [local(): group_block = lax.all_gather(rounded, 'col', axis=0, tiled=True)]
    all_to_all x0 -> x1, blocking collectives: none -> 15.5 us  [match_the_paths(): d_next = lax.all_to_all(v1, axis_name=dev_axis, split_axis=0, concat_axis=0)]
    all_to_all x0 -> x1, waiting for transfers between devices: none -> 14.5 us  [match_the_paths(): d_next = lax.all_to_all(v1, axis_name=dev_axis, split_axis=0, concat_axis=0)]
    all_to_all x0 -> x1, starting transfers between devices: none -> 6.35 us  [match_the_paths(): d_next = lax.all_to_all(v1, axis_name=dev_axis, split_axis=0, concat_axis=0)]
  transfers between devices with their start and end apart: 6 -> 7, of which waited for: 4 -> 5; matrix products, arithmetic and copies ran while one was open for 13% -> 13% of each run, Pallas kernels for 0% -> 0%
where the time goes in v1:
time: 254 us; the launch traced here: 253 us
  waiting for transfers between devices  159 us (63%)
  matrix products  46.9 us (18%)
  between operations  15.8 us (6%)
  blocking collectives  15.5 us (6%)
  starting transfers between devices  6.75 us (3%)
  other arithmetic  5.33 us (2%)
  local copies, waits for them, and re-layouts  3.82 us (2%)
    psum x2, waiting for transfers between devices, broadcast(): return lax.psum(kept, axis)  103 us
    reduce_scatter x2, waiting for transfers between devices, local(): lax.psum_scatter((surface_part + volume_part).astype(jnp.bfloat16), 'col'...  41.2 us
    dot_general x2, matrix products, local(): jnp.dot(surface, column_block, preferred_element_type=jnp.float32)  23.7 us
    all_to_all x1, blocking collectives, match_the_paths(): d_next = lax.all_to_all(v1, axis_name=dev_axis, split_axis=0, concat_axis=0)  15.5 us
    all_to_all x1, waiting for transfers between devices, match_the_paths(): d_next = lax.all_to_all(v1, axis_name=dev_axis, split_axis=0, concat_axis=0)  14.5 us
    dot_general x2, matrix products, local(): lax.dot_general(interp_block, response, (((0,), (0,)), ((), ())), preferr...  9.01 us
    dot_general x2, matrix products, local(): jnp.dot(interp_block, group_block, preferred_element_type=jnp.float32)  8.28 us
    all_to_all x1, starting transfers between devices, match_the_paths(): d_next = lax.all_to_all(v1, axis_name=dev_axis, split_axis=0, concat_axis=0)  6.35 us
  transfers between devices with their start and end apart: 7, of which 5 were waited for; matrix products, arithmetic and copies ran while one was open for 13% of the time, Pallas kernels for 0%

profile of v1, /device:TPU:0, one launch (start us, length us, event | category | flops | bytes accessed | tf_op | source)
XLA Modules:
  0.0 253.1 jit_solution(8476664744811565601)
XLA Ops:
  8.0 0.0 copy-start
  8.0 1.1 convert_element_type.58
  9.1 0.9 stack.4
  10.0 6.3 %all-to-all-start = ((bf16[4,512,128]{2,1,0:T(8,128)(2,1)}), bf16[4,512,128]{2,1,0:T(8,128)(2,1)S(1)}, u32[]{:S(2)}, u32[]{:S(2)}) async-start(bf16[4,512,128]{2,1,0:T(8,128)(2,1)} %stack.4), calls=%async_computation | async-start | bytes 1048576 | tf_op jit(solution)/shard_map/all_to_all | solution.py:14
  16.3 0.0 all-reduce.7.cloned.1.call-start
  16.3 14.5 %all-to-all-done = bf16[4,512,128]{2,1,0:T(8,128)(2,1)S(1)} async-done(((bf16[4,512,128]{2,1,0:T(8,128)(2,1)}), bf16[4,512,128]{2,1,0:T(8,128)(2,1)S(1)}, u32[]{:S(2)}, u32[]{:S(2)}) %all-to-all-start) | async-done | bytes 524320 | tf_op jit(solution)/shard_map/all_to_all | solution.py:14
  30.8 1.1 broadcast_select_fusion.3
  31.9 0.0 copy-start.3
  31.9 0.0 all-reduce.7.cloned.1.call-update
  31.9 0.0 all-gather.5.cloned.1.call-start
  32.0 4.1 %fusion.54 = bf16[1024,128]{1,0:T(8,128)(2,1)} fusion(bf16[2048,128]{1,0:T(8,128)(2,1)S(1)} %bitcast.104, bf16[1,1024,2048]{2,1,0:T(8,128)(2,1)} %param.8), kind=kOutput, calls=%fused_computation.26 | convolution fusion | flops 537001984 | bytes 4980736 | tf_op jit(solution)/shard_map/dot_general | solution.py:41
  36.1 0.0 all-gather.5.cloned.1.call-update
  36.1 0.0 reduce-scatter.3.cloned.1.call-start
  36.2 0.0 copy-done.3
  36.2 0.1 convert_reduce_fusion
  36.3 51.6 %all-reduce.7.cloned.1.call-done = (bf16[2048,128]{1,0:T(8,128)(2,1)}, bf16[2048,128]{1,0:T(8,128)(2,1)}) async-done(((bf16[2048,128]{1,0:T(8,128)(2,1)}, bf16[2048,128]{1,0:T(8,128)(2,1)}), (bf16[2048,128]{1,0:T(8,128)(2,1)}, bf16[2048,128]{1,0:T(8,128)(2,1)})) %all-reduce.7.cloned.1.call-update) | async-done | bytes 1048592 | tf_op jit(solution)/shard_map/psum | solution.py:20
  87.9 0.0 copy-start.1
  88.0 11.9 %fusion.60 = f32[128,2048]{1,0:T(8,128)S(1)} fusion(bf16[2048,4096]{1,0:T(8,128)(2,1)} %param.5, bf16[2048,128]{1,0:T(8,128)(2,1)} %get-tuple-element.8, bf16[2048,128]{1,0:T(8,128)(2,1)} %get-tuple-element.9), kind=kOutput, calls=%fused_computation.28 | convolution fusion | flops 2149580800 | bytes 18874368 | tf_op jit(solution)/shard_map/dot_general | solution.py:54
  99.8 0.0 all-gather.5.cloned.1.call-done
  99.9 2.9 %fusion.70 = f32[1,1024,128]{2,0,1:T(1,128)} fusion(bf16[4,1024,128]{2,1,0:T(8,128)(2,1)} %bitcast.109, bf16[4]{0:T(256)(128)(2,1)S(1)} %convert_reduce_fusion), kind=kOutput, calls=%fused_computation.38 | convolution fusion | flops 1048576 | bytes 1572872 | tf_op jit(solution)/shard_map/p,pmn->mn/dot_general | solution.py:47
  102.8 0.0 copy-done
  102.8 0.0 copy-done.1
  102.8 4.4 %fusion.20 = bf16[2048,128]{0,1:T(8,128)(2,1)} fusion(f32[128,2048]{1,0:T(8,128)S(1)} %fusion.60, bf16[1,1024,2048]{2,1,0:T(8,128)(2,1)} %param.8, bf16[1024,128]{1,0:T(8,128)(2,1)S(1)} %copy-done.1, bf16[1,1024,1024]{2,1,0:T(8,128)(2,1)S(1)} %copy-done, f32[1024,128]{1,0:T(8,128)} %bitcast.108), kind=kOutput, calls=%fused_computation.12 | convolution fusion | flops 806748160 | bytes 8650752 | tf_op jit(solution)/shard_map/dot_general | solution.py:55
  107.2 0.0 reduce-scatter.3.cloned.1.call-update
  107.2 0.0 all-reduce.5.cloned.1.call-start
  107.3 1.1 copy.17
  108.4 20.0 %reduce-scatter.3.cloned.1.call-done = bf16[512,128]{0,1:T(8,128)(2,1)} async-done(((bf16[2048,128]{0,1:T(8,128)(2,1)}), bf16[512,128]{0,1:T(8,128)(2,1)}) %reduce-scatter.3.cloned.1.call-update) | async-done | bytes 131088 | tf_op jit(solution)/shard_map/reduce_scatter | solution.py:58
  128.4 1.0 fusion.88
  129.3 0.1 copy.19
  129.5 0.1 stack.5
  129.6 15.5 %all_to_all.10 = bf16[4,512,128]{2,1,0:T(8,128)(2,1)S(1)} all-to-all(bf16[4,512,128]{2,1,0:T(8,128)(2,1)S(1)} %stack.5), channel_id=1, replica_groups=mesh['row'=8,'col'=4] {'col'}, dimensions={0} | all-to-all | bytes 1048576 | tf_op jit(solution)/shard_map/all_to_all | solution.py:14
  145.1 1.1 broadcast_select_fusion.2
  146.2 0.0 all-reduce.5.cloned.1.call-update
  146.2 0.0 all-gather.7.cloned.1.call-start
  146.2 4.1 %fusion.57 = bf16[128,1024]{0,1:T(8,128)(2,1)} fusion(bf16[2048,128]{1,0:T(8,128)(2,1)S(1)} %bitcast.105, bf16[1,1024,2048]{2,1,0:T(8,128)(2,1)} %param.8), kind=kOutput, calls=%fused_computation.27 | convolution fusion | flops 537001984 | bytes 4980736 | tf_op jit(solution)/shard_map/dot_general | solution.py:41
  150.4 0.0 all-gather.7.cloned.1.call-update
  150.4 0.2 reduce-scatter.5.cloned.1.call-start
  150.6 51.5 %all-reduce.5.cloned.1.call-done = (bf16[2048,128]{1,0:T(8,128)(2,1)}, bf16[2048,128]{1,0:T(8,128)(2,1)}) async-done(((bf16[2048,128]{1,0:T(8,128)(2,1)}, bf16[2048,128]{1,0:T(8,128)(2,1)}), (bf16[2048,128]{1,0:T(8,128)(2,1)}, bf16[2048,128]{1,0:T(8,128)(2,1)})) %all-reduce.5.cloned.1.call-update) | async-done | bytes 1048592 | tf_op jit(solution)/shard_map/psum | solution.py:20
  202.2 11.8 %fusion.64 = f32[128,2048]{1,0:T(8,128)S(1)} fusion(bf16[2048,4096]{1,0:T(8,128)(2,1)} %param.5, bf16[2048,128]{1,0:T(8,128)(2,1)} %get-tuple-element.6, bf16[2048,128]{1,0:T(8,128)(2,1)} %get-tuple-element.7), kind=kOutput, calls=%fused_computation.32 | convolution fusion | flops 2149580800 | bytes 18874368 | tf_op jit(solution)/shard_map/dot_general | solution.py:54
  214.0 0.0 all-gather.7.cloned.1.call-done
  214.0 3.0 %fusion.68 = f32[1,1024,128]{2,0,1:T(1,128)} fusion(bf16[4,1024,128]{2,1,0:T(8,128)(2,1)} %bitcast.110, bf16[4]{0:T(256)(128)(2,1)S(1)} %convert_reduce_fusion), kind=kOutput, calls=%fused_computation.36 | convolution fusion | flops 1048576 | bytes 1572872 | tf_op jit(solution)/shard_map/p,pmn->mn/dot_general | solution.py:47
  217.0 4.6 %fusion.23 = bf16[2048,128]{0,1:T(8,128)(2,1)} fusion(f32[128,2048]{1,0:T(8,128)S(1)} %fusion.64, bf16[1,1024,2048]{2,1,0:T(8,128)(2,1)} %param.8, bf16[128,1024]{0,1:T(8,128)(2,1)} %fusion.57, bf16[1,1024,1024]{2,1,0:T(8,128)(2,1)S(1)} %copy-done, f32[1024,128]{1,0:T(8,128)} %bitcast.107), kind=kOutput, calls=%fused_computation.13 | convolution fusion | flops 806748160 | bytes 8650752 | tf_op jit(solution)/shard_map/dot_general | solution.py:55
  221.6 0.0 reduce-scatter.5.cloned.1.call-update
  221.6 21.2 %reduce-scatter.5.cloned.1.call-done = bf16[512,128]{0,1:T(8,128)(2,1)} async-done(((bf16[2048,128]{0,1:T(8,128)(2,1)}), bf16[512,128]{0,1:T(8,128)(2,1)}) %reduce-scatter.5.cloned.1.call-update) | async-done | bytes 131088 | tf_op jit(solution)/shard_map/reduce_scatter | solution.py:58
  242.8 0.0 copy-done.2
  242.8 1.0 convert_subtract_fusion
  243.8 0.8 copy.22
  244.6 0.8 copy.21
  (2 shorter events, 0.0 us)
Async XLA Ops:
  8.0 94.8 %copy-start = (bf16[1,1024,1024]{2,1,0:T(8,128)(2,1)S(1)}, bf16[1,1024,1024]{2,1,0:T(8,128)(2,1)}, u32[]{:S(2)}) copy-start(bf16[1,1024,1024]{2,1,0:T(8,128)(2,1)} %param.7) | copy-start | bytes 6291460
  10.0 20.8 %all-to-all-start = ((bf16[4,512,128]{2,1,0:T(8,128)(2,1)}), bf16[4,512,128]{2,1,0:T(8,128)(2,1)S(1)}, u32[]{:S(2)}, u32[]{:S(2)}) async-start(bf16[4,512,128]{2,1,0:T(8,128)(2,1)} %stack.4), calls=%async_computation | async-start | bytes 1048576 | tf_op jit(solution)/shard_map/all_to_all | solution.py:14
  16.3 71.6 %all-reduce.7.cloned.1.call-start = ((), (), s32[]{:S(2)}) async-start(), calls=%async_computation.9 | async-start | bytes 2097152 | tf_op jit(solution)/shard_map/psum | solution.py:20
  31.9 4.3 %copy-start.3 = (s32[1,6]{1,0:T(1,128)S(1)}, s32[1,6]{1,0:T(1,128)}, u32[]{:S(2)}) copy-start(s32[1,6]{1,0:T(1,128)} %param.9) | copy-start | bytes 76
  31.9 67.9 %all-gather.5.cloned.1.call-start = ((), (), s32[]{:S(2)}) async-start(), calls=%async_computation.6 | async-start | bytes 1310720 | tf_op jit(solution)/shard_map/all_gather | solution.py:44
  36.1 92.2 %reduce-scatter.3.cloned.1.call-start = ((), (), s32[]{:S(2)}) async-start(), calls=%async_computation.4 | async-start | bytes 655360 | tf_op jit(solution)/shard_map/reduce_scatter | solution.py:58
  87.9 14.9 %copy-start.1 = (bf16[1024,128]{1,0:T(8,128)(2,1)S(1)}, bf16[1024,128]{1,0:T(8,128)(2,1)}, u32[]{:S(2)}) copy-start(bf16[1024,128]{1,0:T(8,128)(2,1)} %fusion.54) | copy-start | bytes 786436
  107.2 94.9 %all-reduce.5.cloned.1.call-start = ((), (), s32[]{:S(2)}) async-start(), calls=%async_computation.8 | async-start | bytes 2097152 | tf_op jit(solution)/shard_map/psum | solution.py:20
  146.2 67.8 %all-gather.7.cloned.1.call-start = ((), (), s32[]{:S(2)}) async-start(), calls=%async_computation.7 | async-start | bytes 1310720 | tf_op jit(solution)/shard_map/all_gather | solution.py:44
  150.4 92.4 %reduce-scatter.5.cloned.1.call-start = ((), (), s32[]{:S(2)}) async-start(), calls=%async_computation.5 | async-start | bytes 655360 | tf_op jit(solution)/shard_map/reduce_scatter | solution.py:58
  217.0 25.8 %copy-start.2 = (bf16[512,128]{0,1:T(8,128)(2,1)S(1)}, bf16[512,128]{0,1:T(8,128)(2,1)}, u32[]{:S(2)}) copy-start(bf16[512,128]{0,1:T(8,128)(2,1)} %reduce-scatter.3.cloned.1.call-done) | copy-start | bytes 393220
Sparse Core Ops, SparseCore 0:
  32.0 55.8 all-reduce.6
  146.3 55.8 all-reduce.4
Sparse Core Ops, SparseCore 1:
  36.2 27.0 all-gather.4
  107.3 21.0 reduce-scatter.2
  150.5 26.9 all-gather.6
  221.7 21.0 reduce-scatter.4
